TPU v7x, 32 devices: a whole 2x2x4 slice. The times are simulated.
32 devices in a mesh: section: 8 (over z, core), board: 4 (over y, x).
Axes of the slice: x: 2, y: 2, z: 4, core: 2. Of those that a mesh axis runs over, the one named last changes fastest.
Arguments:
- root_reach: float32 [2, 8, 1326], replicated, may hold values from 0.05 to 1
- frontier_value: float32 [2, 8, 1326], replicated, may hold values from -60 to 60
- regret_stop: float32 [8, 16, 8, 1326], P('section', 'board'), may hold values from 1 to 30
- regret_go: float32 [8, 16, 8, 1326], P('section', 'board'), may hold values from 1 to 30
- board_live: int32 [16], P('board'), may hold values from 0 to 1, as said below
- board_cards: int32 [16, 5], P('board'), may hold values from 0 to 51, as said below
- hand_rank: int32 [16, 1326], P('board'), may hold values from 0 to 1325
Outputs:
- new_stop: float32 [8, 16, 8, 1326], P('section', 'board')
- new_go: float32 [8, 16, 8, 1326], P('section', 'board')
- section_values: float32 [8, 2, 8, 1326], P('section')
Inputs may be any that keep to these rules, and one draw needn't show every extreme that they name: `board_live`: 0 or 1; among each device's 4 slots the first one is always 1. `board_cards`: a slot's 5 cards are distinct. `hand_rank`: equal values tie.
All inputs are finite; a program needn't handle non-finite values.
Results may differ from a plain program's by a relative error of at most 0.0008.
Values sent between devices are 32-bit elements; how exact they have to be, the bound alone decides.
A program may use at most 64 MiB of HBM per device.

v0:
```python
import jax
import jax.numpy as jnp
import numpy as np
from jax import lax
from jax.sharding import PartitionSpec as P

CARDS = 52


def free_pairs():
    first, second = np.triu_indices(CARDS, 1)
    first = jnp.asarray(first.astype(np.int32))
    second = jnp.asarray(second.astype(np.int32))
    shared = (
        (first[:, None] == first[None, :])
        | (first[:, None] == second[None, :])
        | (second[:, None] == first[None, :])
        | (second[:, None] == second[None, :])
    )
    return jnp.where(shared, 0.0, 1.0).astype(jnp.bfloat16)


def board_masks(board_cards):
    first, second = np.triu_indices(CARDS, 1)
    first = jnp.asarray(first.astype(np.int32))
    second = jnp.asarray(second.astype(np.int32))
    hits = (board_cards[:, :, None] == first[None, None, :]) | (
        board_cards[:, :, None] == second[None, None, :]
    )
    return jnp.where(jnp.any(hits, axis=1), 0.0, 1.0).astype(jnp.float32)


def showdown(reach_one, stop_weight, mask_row, rank_row, disjoint):
    leaf_reach = (reach_one * stop_weight).astype(jnp.bfloat16)
    mask_half = mask_row.astype(jnp.bfloat16)
    payoff = (
        jnp.sign(rank_row[:, None] - rank_row[None, :]).astype(jnp.bfloat16)
        * disjoint
        * mask_half[:, None]
        * mask_half[None, :]
    )
    flipped = leaf_reach[::-1].reshape(-1, leaf_reach.shape[-1])
    result = jnp.einsum("rk,hk->rh", flipped, payoff, preferred_element_type=jnp.float32)
    return result.reshape(leaf_reach.shape)


def local(root_reach, frontier_value, regret_stop, regret_go, board_live, board_cards, hand_rank):
    section_idx = lax.axis_index("section")
    players = jnp.arange(2)[:, None, None]
    acting = players == section_idx % 2
    masks = board_masks(board_cards)
    alive = board_live > 0
    alive_weight = alive.astype(jnp.float32)
    stop_now = regret_stop[0]
    go_now = regret_go[0]
    regret_sum = stop_now + go_now
    stop_prob = stop_now / regret_sum
    go_prob = go_now / regret_sum
    factor = jnp.where(acting[None], go_prob[:, None], 1.0)
    stop_weight = jnp.where(acting[None], stop_prob[:, None], 1.0)
    root_masked = root_reach[None] * masks[:, None, None, :]
    factor_all = lax.all_gather(factor[None], "section", axis=0, tiled=True)
    levels = jnp.arange(factor_all.shape[0])[:, None, None, None, None]
    reach_now = root_masked * jnp.prod(jnp.where(levels < section_idx, factor_all, 1.0), axis=0)
    disjoint = free_pairs()
    leaf_list = []
    for slot in range(masks.shape[0]):
        leaf_one = showdown(
            reach_now[slot], stop_weight[slot], masks[slot], hand_rank[slot], disjoint
        )
        leaf_list.append(leaf_one)
    leaf_values = jnp.stack(leaf_list)
    weighted = stop_weight * leaf_values
    frontier_masked = frontier_value[None] * masks[:, None, None, :]
    leaf_all = lax.all_gather(weighted[None], "section", axis=0, tiled=True)
    section_total = leaf_all.shape[0]

    def climb(position, carried):
        level_now = section_total - 1 - position
        updated = leaf_all[level_now] + factor_all[level_now] * carried
        return jnp.where(level_now > section_idx, updated, carried)

    value_next = lax.fori_loop(0, section_total, climb, frontier_masked)
    node_value = weighted + factor * value_next
    section_part = jnp.sum(alive_weight[:, None, None, None] * node_value, axis=0)
    live_part = jnp.sum(alive_weight)
    section_sum, live_total = lax.psum((section_part, live_part), "board")
    section_value = section_sum / live_total
    own_next = jnp.sum(jnp.where(acting[None], value_next, 0.0), axis=1)
    own_leaf = jnp.sum(jnp.where(acting[None], leaf_values, 0.0), axis=1)
    gap = own_leaf - own_next
    keep_slot = alive[:, None, None]
    new_stop = jnp.where(keep_slot, jnp.maximum(stop_now + go_prob * gap, 0.0), stop_now)
    new_go = jnp.where(keep_slot, jnp.maximum(go_now - stop_prob * gap, 0.0), go_now)
    return (new_stop[None], new_go[None], section_value[None])


def solution(mesh):
    return jax.shard_map(
        local,
        mesh=mesh,
        in_specs=(
            P(),
            P(),
            P("section", "board", None, None),
            P("section", "board", None, None),
            P("board"),
            P("board", None),
            P("board", None),
        ),
        out_specs=(
            P("section", "board", None, None),
            P("section", "board", None, None),
            P("section", None, None, None),
        ),
        check_vma=False,
    )
```

profile of v0, /device:TPU:0, one launch (start us, length us, event | category | flops | bytes accessed | tf_op | source)
XLA Modules:
  0.0 163.7 jit_solution(3219703104629716634)
XLA Ops:
  7.3 1.0 add_divide_fusion.1
  8.3 0.8 broadcast_select_fusion.1
  9.2 0.8 copy.14
  10.0 0.8 or_reduce_fusion
  10.8 0.1 fusion.53
  10.9 0.9 slice_reduce_fusion.3
  11.9 0.1 broadcast_select_fusion
  12.0 36.4 %all-gather.3.cloned.1.call-done = f32[8,4,2,8,1326]{4,3,2,1,0:T(8,128)} async-done(((f32[1,4,2,8,1326]{4,3,2,1,0:T(8,128)}), f32[8,4,2,8,1326]{4,3,2,1,0:T(8,128)}) %all-gather.3.cloned.1.call-update) | async-done | bytes 2715664 | tf_op jit(solution)/shard_map/all_gather | solution.py:62
  48.3 2.1 %select_reduce_fusion = f32[4,2,8,1326]{3,2,1,0:T(8,128)S(1)} fusion(f32[8,4,2,8,1326]{4,3,2,1,0:T(8,128)} %all-gather.3.cloned.1.call-done, pred[8]{0:T(512)(128)(4,1)S(1)} %iota_compare_fusion), kind=kLoop, calls=%fused_computation.28 | loop fusion | flops 1272960 | bytes 3055112 | tf_op jit(solution)/shard_map/reduce_prod | solution.py:64
  50.5 0.1 multiply_multiply_fusion
  50.6 0.1 fusion.46
  50.7 3.7 %fusion.24 = f32[2,8,1326]{2,1,0:T(8,128)S(1)} fusion(bf16[2,8,1326]{2,1,0:T(8,128)(2,1)S(1)} %rev.12, s32[1326]{0:T(1024)S(1)} %get-tuple-element.143, s32[1326]{0:T(1024)S(1)} %copy-done.5, s32[1326]{0:T(1024)S(1)} %copy-done.4, bf16[1326]{0:T(1024)(128)(2,1)S(1)} %get-tuple-element.139), kind=kOutput, calls=%fused_computation.27 | convolution fusion | flops 91430352 | bytes 145860 | tf_op jit(solution)/shard_map/rk,hk->rh/dot_general | solution.py:43
  54.4 3.7 %fusion.22 = f32[2,8,1326]{2,1,0:T(8,128)S(1)} fusion(bf16[2,8,1326]{2,1,0:T(8,128)(2,1)S(1)} %rev.13, s32[1326]{0:T(1024)S(1)} %get-tuple-element.144, s32[1326]{0:T(1024)S(1)} %copy-done.5, s32[1326]{0:T(1024)S(1)} %copy-done.4, bf16[1326]{0:T(1024)(128)(2,1)S(1)} %get-tuple-element.142), kind=kOutput, calls=%fused_computation.26 | convolution fusion | flops 91430352 | bytes 145860 | tf_op jit(solution)/shard_map/rk,hk->rh/dot_general | solution.py:43
  58.1 3.7 %fusion.20 = f32[2,8,1326]{2,1,0:T(8,128)S(1)} fusion(bf16[2,8,1326]{2,1,0:T(8,128)(2,1)S(1)} %rev.14, s32[1326]{0:T(1024)S(1)} %get-tuple-element.146, s32[1326]{0:T(1024)S(1)} %copy-done.5, s32[1326]{0:T(1024)S(1)} %copy-done.4, bf16[1326]{0:T(1024)(128)(2,1)S(1)} %get-tuple-element.141), kind=kOutput, calls=%fused_computation.25 | convolution fusion | flops 91430352 | bytes 145860 | tf_op jit(solution)/shard_map/rk,hk->rh/dot_general | solution.py:43
  61.8 3.9 %fusion.18 = f32[2,8,1326]{2,1,0:T(8,128)S(1)} fusion(bf16[2,8,1326]{2,1,0:T(8,128)(2,1)S(1)} %rev.15, s32[1326]{0:T(1024)S(1)} %get-tuple-element.145, s32[1326]{0:T(1024)S(1)} %copy-done.5, s32[1326]{0:T(1024)S(1)} %copy-done.4, bf16[1326]{0:T(1024)(128)(2,1)S(1)} %get-tuple-element.140), kind=kOutput, calls=%fused_computation.24 | convolution fusion | flops 91430352 | bytes 145860 | tf_op jit(solution)/shard_map/rk,hk->rh/dot_general | solution.py:43
  65.7 0.8 maximum_multiply_fusion
  66.6 0.6 convert_reduce_fusion
  67.2 10.5 %psum.15 = f32[]{:T(128)} all-reduce(f32[]{:T(128)} %convert_reduce_fusion), channel_id=1, replica_groups=mesh['section'=8,'board'=4] {'board'}, use_global_device_ids=true, to_apply=%region_9.10 | all-reduce | flops 1 | bytes 8 | tf_op jit(solution)/shard_map/psum | solution.py:87
  77.8 23.9 %all-gather.5.cloned.1.call-done = f32[8,4,2,8,1326]{4,3,2,1,0:T(8,128)} async-done(((f32[1,4,2,8,1326]{4,3,2,1,0:T(8,128)}), f32[8,4,2,8,1326]{4,3,2,1,0:T(8,128)}) %all-gather.5.cloned.1.call-update) | async-done | bytes 2715664 | tf_op jit(solution)/shard_map/all_gather | solution.py:75
  101.7 11.1 %while.15 = (s32[]{:T(128)}, f32[4,2,8,1326]{3,2,1,0:T(8,128)S(1)}, s32[]{:T(128)}, f32[8,4,2,8,1326]{4,3,2,1,0:T(8,128)}, f32[8,4,2,8,1326]{4,3,2,1,0:T(8,128)}...) while((s32[]{:T(128)}, f32[4,2,8,1326]{3,2,1,0:T(8,128)S(1)}, s32[]{:T(128)}, ...), condition=%wide.region_4.5_spmd, body=%wide.region_3.4_spmd.sunk | while | flops 254599 | bytes 1357977 | solution.py:83
  101.7 1.4 fusion.68
  103.1 1.4 fusion.68
  104.5 1.4 fusion.68
  105.9 1.4 fusion.68
  107.3 1.4 fusion.68
  108.7 1.4 fusion.68
  110.1 1.4 fusion.68
  111.5 1.4 fusion.68
  112.8 0.9 multiply_reduce_fusion
  113.7 0.8 fusion.41
  114.6 40.3 %all-reduce.2.cloned.1.call-done = f32[2,8,1326]{2,1,0:T(8,128)} async-done(((f32[2,8,1326]{2,1,0:T(8,128)}), f32[2,8,1326]{2,1,0:T(8,128)}) %all-reduce.2.cloned.1.call-update) | async-done | bytes 84880 | tf_op jit(solution)/shard_map/psum | solution.py:87
  154.9 2.2 %divide_bitcast_fusion = f32[1,2,8,1326]{3,2,1,0:T(8,128)} fusion(f32[2,8,1326]{2,1,0:T(8,128)} %all-reduce.2.cloned.1.call-done, f32[]{:T(128)} %psum.15), kind=kLoop, calls=%fused_computation.67 | loop fusion | flops 21216 | bytes 169732 | tf_op jit(solution)/shard_map/broadcast_in_dim | solution.py:95
  (28 shorter events, 0.3 us)
Async XLA Ops:
  7.2 43.3 %copy-start.2 = (f32[2,8,1326]{2,1,0:T(8,128)S(1)}, f32[2,8,1326]{2,1,0:T(8,128)}, u32[]{:S(2)}) copy-start(f32[2,8,1326]{2,1,0:T(8,128)} %param.13) | copy-start | bytes 254596
  7.2 43.3 %copy-start.3 = (f32[2,8,1326]{2,1,0:T(8,128)S(1)}, f32[2,8,1326]{2,1,0:T(8,128)}, u32[]{:S(2)}) copy-start(f32[2,8,1326]{2,1,0:T(8,128)} %param.14) | copy-start | bytes 254596
  7.2 41.2 %all-gather.3.cloned.1.call-start = ((), (), s32[]{:S(2)}) async-start(), calls=%async_computation | async-start | bytes 3244032 | tf_op jit(solution)/shard_map/all_gather | solution.py:62
  9.2 92.5 %all-gather.5.cloned.1.call-start = ((), (), s32[]{:S(2)}) async-start(), calls=%async_computation.1 | async-start | bytes 3244032 | tf_op jit(solution)/shard_map/all_gather | solution.py:75
  12.0 38.7 %copy-start.4 = (s32[1326]{0:T(1024)S(1)}, s32[1326]{0:T(1024)}, u32[]{:S(2)}) copy-start(s32[1326]{0:T(1024)} %constant.74.clone) | copy-start | bytes 15916
  12.0 38.7 %copy-start.5 = (s32[1326]{0:T(1024)S(1)}, s32[1326]{0:T(1024)}, u32[]{:S(2)}) copy-start(s32[1326]{0:T(1024)} %constant.75.clone) | copy-start | bytes 15916
  61.8 4.8 %copy-start.6 = (s32[4]{0:T(128)S(1)}, s32[4]{0:T(128)}, u32[]{:S(2)}) copy-start(s32[4]{0:T(128)} %param.17) | copy-start | bytes 52
  66.6 88.3 %all-reduce.2.cloned.1.call-start = ((), (), s32[]{:S(2)}) async-start(), calls=%async_computation.2 | async-start | bytes 180224 | tf_op jit(solution)/shard_map/psum | solution.py:87
  101.7 12.0 %copy-start = (f32[1,4,8,1326]{3,2,1,0:T(8,128)S(1)}, f32[1,4,8,1326]{3,2,1,0:T(8,128)}, u32[]{:S(2)}) copy-start(f32[1,4,8,1326]{3,2,1,0:T(8,128)} %param.16) | copy-start | bytes 509188
  101.7 12.0 %copy-start.1 = (f32[1,4,8,1326]{3,2,1,0:T(8,128)S(1)}, f32[1,4,8,1326]{3,2,1,0:T(8,128)}, u32[]{:S(2)}) copy-start(f32[1,4,8,1326]{3,2,1,0:T(8,128)} %param.15) | copy-start | bytes 509188
Sparse Core Ops, SparseCore 0:
  9.6 38.6 all-gather.2
  66.7 34.9 all-gather.4
  113.8 41.0 all-reduce.1
where the time goes:
time: 164 us
  waiting for transfers between devices  101 us (62%)
  other arithmetic  21.4 us (13%)
  matrix products  15 us (9%)
  between operations  13.9 us (8%)
  blocking collectives  10.5 us (6%)
  local copies, waits for them, and re-layouts  1.84 us (1%)
    psum x1, waiting for transfers between devices, local(): section_sum, live_total = lax.psum((section_part, live_part), 'board')  40.3 us
    all_gather x1, waiting for transfers between devices, local(): factor_all = lax.all_gather(factor[None], 'section', axis=0, tiled=True)  36.4 us
    all_gather x1, waiting for transfers between devices, local(): leaf_all = lax.all_gather(weighted[None], 'section', axis=0, tiled=True)  23.9 us
    dot_general x4, matrix products, showdown(): jnp.einsum('rk,hk->rh', flipped, payoff, preferred_element_type=jnp.float32)  15 us
    select_n x8, other arithmetic, climb(): return jnp.where(level_now > section_idx, updated, carried)  10.9 us
    psum x1, blocking collectives, local(): section_sum, live_total = lax.psum((section_part, live_part), 'board')  10.5 us
  transfers between devices with their start and end apart: 3, of which 3 were waited for; matrix products, arithmetic and copies ran while one was open for 3% of the time, Pallas kernels for 0%

commit v1 on v0

v1 whole, which is shorter than its diff:
```python
import functools

import jax
import jax.numpy as jnp
import numpy as np
from jax import lax
from jax.experimental import pallas as pl
from jax.experimental.pallas import tpu as pltpu
from jax.sharding import PartitionSpec as P

CARDS = 52
LANES = 128
MESH = pl.DeviceIdType.MESH


def pair_tables(hands, width):
    first, second = np.triu_indices(CARDS, 1)
    cards = np.full((8, width), -1, np.int32)
    cards[0, :hands] = first
    cards[1, :hands] = second
    holds = np.zeros((width, LANES), np.float32)
    holds[np.arange(hands), first] = 1.0
    holds[np.arange(hands), second] = 1.0
    left = -holds
    left[:hands, CARDS] = 1.0
    right = holds.T.copy()
    right[CARDS, :hands] = 1.0
    return (
        jnp.asarray(cards),
        jnp.asarray(left, jnp.bfloat16),
        jnp.asarray(right, jnp.bfloat16),
    )


def kernel(
    sizes,
    root_ref,
    frontier_ref,
    stop_ref,
    go_ref,
    live_ref,
    board_ref,
    rank_ref,
    cards_ref,
    left_ref,
    right_ref,
    new_stop_ref,
    new_go_ref,
    value_ref,
    go_send,
    go_recv,
    gap_send,
    gap_recv,
    sum_send,
    sum_recv,
    part_send,
    part_recv,
    free_pairs,
    payoff,
    reach_rows,
    leaf_rows,
    gap_home,
    send1,
    recv1,
    send2,
    recv2,
    send3,
    recv3,
    send4,
    recv4,
):
    depths, groups, boards, nodes, hands, width, chunk = sizes
    me = lax.axis_index("section")
    group = lax.axis_index("board")
    barrier = pltpu.get_barrier_semaphore()
    for step in range(1, depths):
        peer = lax.rem(me + step, depths)
        pl.semaphore_signal(barrier, inc=1, device_id={"section": peer}, device_id_type=MESH)
    for step in range(1, groups):
        peer = lax.rem(group + step, groups)
        pl.semaphore_signal(barrier, inc=1, device_id={"board": peer}, device_id_type=MESH)

    tail = width - LANES
    go_send[:, :, tail:] = jnp.zeros((depths, chunk, LANES), jnp.float32)
    for j in range(boards):
        stop_now = stop_ref[j]
        go_now = go_ref[j]
        go_prob = go_now / (stop_now + go_now)
        for n in range(nodes):
            unit = n * boards + j
            go_send[unit // chunk, unit % chunk : unit % chunk + 1, :hands] = go_prob[n : n + 1]

    pl.semaphore_wait(barrier, depths - 1 + groups - 1)

    def go_copy(target):
        return pltpu.make_async_remote_copy(
            src_ref=go_send.at[target],
            dst_ref=go_recv.at[me],
            send_sem=send1.at[target],
            recv_sem=recv1.at[me],
            device_id={"section": target},
            device_id_type=MESH,
        )

    def go_arrival(source):
        return pltpu.make_async_remote_copy(
            src_ref=go_send.at[source],
            dst_ref=go_recv.at[source],
            send_sem=send1.at[source],
            recv_sem=recv1.at[source],
            device_id={"section": source},
            device_id_type=MESH,
        )

    for step in range(1, depths):
        go_copy(lax.rem(me + step, depths)).start()
    go_recv[me] = go_send[me]

    node = (me * chunk) // boards
    block = lax.rem(me, boards // chunk)
    rank = rank_ref[block].astype(jnp.float32)
    rank = jnp.concatenate(
        [rank, jnp.zeros((chunk, width - hands), jnp.float32)], axis=1
    )
    rank = jnp.concatenate([rank, jnp.zeros((8 - chunk, width), jnp.float32)], axis=0)
    rank_col = jnp.transpose(rank)
    free_pairs[...] = jnp.maximum(
        jnp.dot(left_ref[...], right_ref[...], preferred_element_type=jnp.float32), 0.0
    ).astype(jnp.bfloat16)
    for i in range(chunk):
        for top in range(0, width, LANES):
            diff = rank[i : i + 1, :] - rank_col[top : top + LANES, i : i + 1]
            sign = jnp.clip(diff, -1.0, 1.0).astype(jnp.bfloat16)
            payoff[i, top : top + LANES, :] = sign * free_pairs[top : top + LANES, :]

    lane = lax.broadcasted_iota(jnp.int32, (chunk, width), 1)
    mask = lane < hands
    cards = board_ref[block]
    for m in range(cards.shape[1]):
        card = cards[:, m : m + 1]
        mask = mask & (cards_ref[0:1, :] != card) & (cards_ref[1:2, :] != card)
    mask = jnp.where(mask, 1.0, 0.0)

    pad = jnp.zeros((1, width - hands), jnp.float32)

    def node_row(ref, player):
        return jnp.concatenate([ref[player, pl.ds(node, 1), :], pad], axis=1) * mask

    reach = [node_row(root_ref, p) for p in range(2)]

    for step in range(1, depths):
        go_arrival(lax.rem(me + depths - step, depths)).wait_recv()

    for t in range(depths):
        q = t % 2
        go_t = go_recv[t]
        weighted = [reach[0], reach[1]]
        weighted[q] = reach[q] * (1.0 - go_t)
        for p in range(2):
            for i in range(chunk):
                row = p * depths + t
                reach_rows[i, row : row + 1, :] = weighted[1 - p][i : i + 1]
        reach[q] = reach[q] * go_t
    for i in range(chunk):
        leaf_rows[i] = jnp.dot(
            reach_rows[i].astype(jnp.bfloat16),
            payoff[i],
            preferred_element_type=jnp.float32,
        )

    def gap_copy(target, source):
        return pltpu.make_async_remote_copy(
            src_ref=gap_send.at[target],
            dst_ref=gap_recv.at[source],
            send_sem=send2.at[target],
            recv_sem=recv2.at[source],
            device_id={"section": target},
            device_id_type=MESH,
        )

    def sum_copy(target, source):
        return pltpu.make_async_remote_copy(
            src_ref=sum_send.at[target],
            dst_ref=sum_recv.at[source],
            send_sem=send3.at[target],
            recv_sem=recv3.at[source],
            device_id={"section": target},
            device_id_type=MESH,
        )

    value = [node_row(frontier_ref, p) for p in range(2)]
    alive = [
        jnp.where(live_ref[block * chunk + i] > 0, 1.0, 0.0) for i in range(chunk)
    ]
    for t in reversed(range(depths)):
        q = t % 2
        go_t = go_recv[t]
        leaf = [
            jnp.concatenate(
                [leaf_rows[i, p * depths + t : p * depths + t + 1, :] for i in range(chunk)],
                axis=0,
            )
            * mask
            for p in range(2)
        ]
        gap_send[t] = leaf[q] - value[q]
        value[q] = (1.0 - go_t) * leaf[q] + go_t * value[q]
        value[1 - q] = leaf[1 - q] + value[1 - q]
        for p in range(2):
            total = alive[0] * value[p][0:1]
            for i in range(1, chunk):
                total = total + alive[i] * value[p][i : i + 1]
            sum_send[t, p : p + 1, :] = total

        @pl.when(t != me)
        def _():
            gap_copy(t, me).start()
            sum_copy(t, me).start()

    gap_recv[me] = gap_send[me]
    sum_recv[me] = sum_send[me]

    for step in range(1, depths):
        sum_copy(0, lax.rem(me + depths - step, depths)).wait_recv()
    per_node = boards // chunk
    for n in range(nodes):
        for p in range(2):
            total = sum_recv[n * per_node, p : p + 1, :]
            for extra in range(1, per_node):
                total = total + sum_recv[n * per_node + extra, p : p + 1, :]
            part_send[p, n : n + 1, :] = total
    live_count = jnp.where(live_ref[0] > 0, 1.0, 0.0)
    for j in range(1, boards):
        live_count = live_count + jnp.where(live_ref[j] > 0, 1.0, 0.0)
    part_send[:, :, hands:] = jnp.full((2, nodes, width - hands), 1.0, jnp.float32) * live_count

    def part_copy(target, source):
        return pltpu.make_async_remote_copy(
            src_ref=part_send,
            dst_ref=part_recv.at[source],
            send_sem=send4.at[target],
            recv_sem=recv4.at[source],
            device_id={"board": target},
            device_id_type=MESH,
        )

    for step in range(1, groups):
        part_copy(lax.rem(group + step, groups), group).start()
    part_recv[group] = part_send[...]

    for step in range(1, depths):
        gap_copy(0, lax.rem(me + depths - step, depths)).wait_recv()
    for k in range(depths):
        for i in range(chunk):
            unit = k * chunk + i
            n, j = unit // boards, unit % boards
            gap_home[j, n : n + 1, :] = gap_recv[k, i : i + 1, :]
    for j in range(boards):
        stop_now = stop_ref[j]
        go_now = go_ref[j]
        total = stop_now + go_now
        keep = live_ref[j] > 0
        gap = gap_home[j][:, :hands]
        new_stop = jnp.maximum(stop_now + (go_now / total) * gap, 0.0)
        new_go = jnp.maximum(go_now - (stop_now / total) * gap, 0.0)
        new_stop_ref[j] = jnp.where(keep, new_stop, stop_now)
        new_go_ref[j] = jnp.where(keep, new_go, go_now)

    for step in range(1, groups):
        part_copy(0, lax.rem(group + groups - step, groups)).wait_recv()
    for p in range(2):
        total = part_recv[0, p]
        for b in range(1, groups):
            total = total + part_recv[b, p]
        value_ref[p] = total[:, :hands] / total[:, hands : hands + 1]

    for step in range(1, depths):
        peer = lax.rem(me + step, depths)
        go_copy(peer).wait_send()
        gap_copy(peer, me).wait_send()
        sum_copy(peer, me).wait_send()
    for step in range(1, groups):
        part_copy(lax.rem(group + step, groups), group).wait_send()


def local(depths, groups, root, frontier, regret_stop, regret_go, live, board_cards, rank):
    boards, nodes, hands = regret_stop.shape[1:]
    width = -(-hands // LANES) * LANES
    chunk = nodes * boards // depths
    sizes = (depths, groups, boards, nodes, hands, width, chunk)
    cards, left, right = pair_tables(hands, width)
    vmem = pl.BlockSpec(memory_space=pltpu.VMEM)
    smem = pl.BlockSpec(memory_space=pltpu.SMEM)
    f32 = jnp.float32
    dma = pltpu.SemaphoreType.DMA
    outs = pl.pallas_call(
        functools.partial(kernel, sizes),
        out_shape=(
            jax.ShapeDtypeStruct((boards, nodes, hands), f32),
            jax.ShapeDtypeStruct((boards, nodes, hands), f32),
            jax.ShapeDtypeStruct((2, nodes, hands), f32),
        ),
        in_specs=[vmem] * 4 + [smem] + [vmem] * 5,
        out_specs=(vmem, vmem, vmem),
        scratch_shapes=[
            pltpu.VMEM((depths, chunk, width), f32),
            pltpu.VMEM((depths, chunk, width), f32),
            pltpu.VMEM((depths, chunk, width), f32),
            pltpu.VMEM((depths, chunk, width), f32),
            pltpu.VMEM((depths, 2, width), f32),
            pltpu.VMEM((depths, 2, width), f32),
            pltpu.VMEM((2, nodes, width), f32),
            pltpu.VMEM((groups, 2, nodes, width), f32),
            pltpu.VMEM((width, width), jnp.bfloat16),
            pltpu.VMEM((chunk, width, width), jnp.bfloat16),
            pltpu.VMEM((chunk, 2 * depths, width), f32),
            pltpu.VMEM((chunk, 2 * depths, width), f32),
            pltpu.VMEM((boards, nodes, width), f32),
            dma((depths,)),
            dma((depths,)),
            dma((depths,)),
            dma((depths,)),
            dma((depths,)),
            dma((depths,)),
            dma((groups,)),
            dma((groups,)),
        ],
        compiler_params=pltpu.CompilerParams(
            collective_id=0, has_side_effects=True, vmem_limit_bytes=56 * 1024 * 1024
        ),
    )(
        root,
        frontier,
        regret_stop[0],
        regret_go[0],
        live,
        board_cards.reshape(boards // chunk, chunk, -1),
        rank.reshape(boards // chunk, chunk, hands),
        cards,
        left,
        right,
    )
    return tuple(out[None] for out in outs)


def solution(mesh):
    return jax.shard_map(
        functools.partial(local, mesh.shape["section"], mesh.shape["board"]),
        mesh=mesh,
        in_specs=(
            P(),
            P(),
            P("section", "board", None, None),
            P("section", "board", None, None),
            P("board"),
            P("board", None),
            P("board", None),
        ),
        out_specs=(
            P("section", "board", None, None),
            P("section", "board", None, None),
            P("section", None, None, None),
        ),
        check_vma=False,
    )
```

time: 164 us -> 33.1 us (0.20)
  waiting for transfers between devices: 101 us -> 0 us
  Pallas kernels: 0 us -> 29 us
  other arithmetic: 21.4 us -> 0 us
  matrix products: 15 us -> 0 us
  between operations: 13.9 us -> 0.65 us
  blocking collectives: 10.5 us -> 0 us
    all_gather x2 -> x0, waiting for transfers between devices: 60.3 us -> none  [the longest x1 36.4 us: local(): factor_all = lax.all_gather(factor[None], 'section', axis=0, tiled=True)]
    psum x1 -> x0, waiting for transfers between devices: 40.3 us -> none  [local(): section_sum, live_total = lax.psum((section_part, live_part), 'board')]
    pallas_call x0 -> x1, Pallas kernels: none -> 29 us  [local(): pl.pallas_call(functools.partial(kernel, sizes), out_shape=(jax.ShapeDtyp...]
    dot_general x4 -> x0, matrix products: 15 us -> none  [showdown(): jnp.einsum('rk,hk->rh', flipped, payoff, preferred_element_type=jnp.float32)]
    select_n x12 -> x0, other arithmetic: 12.7 us -> none  [the longest x8 10.9 us: climb(): return jnp.where(level_now > section_idx, updated, carried)]
    psum x1 -> x0, blocking collectives: 10.5 us -> none  [local(): section_sum, live_total = lax.psum((section_part, live_part), 'board')]
    unnamed x15 -> x7, local copies, waits for them, and re-layouts: 0.8 us -> 3.22 us
    broadcast_in_dim x1 -> x0, other arithmetic: 2.23 us -> none  [local(): return (new_stop[None], new_go[None], section_value[None])]
  transfers between devices with their start and end apart: 3 -> 0, of which waited for: 3 -> 0; matrix products, arithmetic and copies ran while one was open for 3% -> 0% of each run, Pallas kernels for 0% -> 0%
where the time goes in v1:
time: 33.1 us; the launch traced here: 32.9 us
  Pallas kernels  29 us (88%)
  local copies, waits for them, and re-layouts  3.22 us (10%)
  between operations  0.65 us (2%)
    pallas_call x1, Pallas kernels, local(): pl.pallas_call(functools.partial(kernel, sizes), out_shape=(jax.ShapeDtyp...  29 us
    unnamed x7, local copies, waits for them, and re-layouts  3.22 us

profile of v1, /device:TPU:0, one launch (start us, length us, event | category | flops | bytes accessed | tf_op | source)
XLA Modules:
  0.0 32.9 jit_solution(4411725857684426360)
XLA Ops:
  0.6 29.0 %shard_map.121 = (f32[4,8,1326]{2,1,0:T(8,128)}, f32[4,8,1326]{2,1,0:T(8,128)}, f32[2,8,1326]{2,1,0:T(8,128)}) custom-call(f32[2,8,1326]{2,1,0:T(8,128)} %root_ref.1, f32[2,8,1326]{2,1,0:T(8,128)} %frontier_ref.1, f32[4,8,1326]{2,1,0:T(8,128)} %bitcast.7, f32[4,8,1326]{2,1,0:T(8,128)} %bitcast.8, s32[4]{0:T(128)} %live_ref.1, s32[1,4,5]{2,1,0:T(4,128)} %bitcast.13, ...), custom_call_target="tpu_custom_call" | custom-call | tf_op jit(solution)/shard_map/pallas_call | solution.py:296
  29.7 0.0 copy-start
  29.7 1.6 %copy.16 = f32[1,4,8,1326]{3,2,1,0:T(8,128)} copy(f32[1,4,8,1326]{3,2,1,0:T(8,128)} %bitcast.10) | data formatting | bytes 339456
  31.3 0.0 copy-done
  31.3 0.0 copy-start.1
  31.3 0.7 %copy.17 = f32[1,4,8,1326]{3,2,1,0:T(8,128)} copy(f32[1,4,8,1326]{3,2,1,0:T(8,128)S(1)} %bitcast.9) | data formatting | bytes 339456
  32.0 0.3 copy-done.1
  32.3 0.6 %copy.18 = f32[1,2,8,1326]{3,2,1,0:T(8,128)} copy(f32[1,2,8,1326]{3,2,1,0:T(8,128)S(1)} %bitcast.11) | data formatting | bytes 169728
Async XLA Ops:
  29.7 1.7 %copy-start = (f32[4,8,1326]{2,1,0:T(8,128)S(1)}, f32[4,8,1326]{2,1,0:T(8,128)}, u32[]{:S(2)}) copy-start(f32[4,8,1326]{2,1,0:T(8,128)} %get-tuple-element.7) | copy-start | bytes 509188
  31.3 0.9 %copy-start.1 = (f32[2,8,1326]{2,1,0:T(8,128)S(1)}, f32[2,8,1326]{2,1,0:T(8,128)}, u32[]{:S(2)}) copy-start(f32[2,8,1326]{2,1,0:T(8,128)} %get-tuple-element.8) | copy-start | bytes 254596

commit v2 on v1

--- a/solution.py
+++ b/solution.py
@@ -34,6 +34,19 @@
 
 def kernel(
     sizes,
+    root_hbm,
+    frontier_hbm,
+    stop_hbm,
+    go_hbm,
+    live_hbm,
+    board_hbm,
+    rank_hbm,
+    cards_hbm,
+    left_hbm,
+    right_hbm,
+    new_stop_ref,
+    new_go_ref,
+    value_ref,
     root_ref,
     frontier_ref,
     stop_ref,
@@ -44,9 +57,7 @@
     cards_ref,
     left_ref,
     right_ref,
-    new_stop_ref,
-    new_go_ref,
-    value_ref,
+    fetch_sem,
     go_send,
     go_recv,
     gap_send,
@@ -80,8 +91,21 @@
         peer = lax.rem(group + step, groups)
         pl.semaphore_signal(barrier, inc=1, device_id={"board": peer}, device_id_type=MESH)
 
+    sources = (stop_hbm, go_hbm, rank_hbm, left_hbm, right_hbm)
+    sources += (cards_hbm, board_hbm, root_hbm, frontier_hbm, live_hbm)
+    places = (stop_ref, go_ref, rank_ref, left_ref, right_ref)
+    places += (cards_ref, board_ref, root_ref, frontier_ref, live_ref)
+    fetches = [
+        pltpu.make_async_copy(source, place, fetch_sem.at[at])
+        for at, (source, place) in enumerate(zip(sources, places))
+    ]
+    for fetch in fetches:
+        fetch.start()
+
     tail = width - LANES
     go_send[:, :, tail:] = jnp.zeros((depths, chunk, LANES), jnp.float32)
+    fetches[0].wait()
+    fetches[1].wait()
     for j in range(boards):
         stop_now = stop_ref[j]
         go_now = go_ref[j]
@@ -115,6 +139,9 @@
     for step in range(1, depths):
         go_copy(lax.rem(me + step, depths)).start()
     go_recv[me] = go_send[me]
+
+    for fetch in fetches[2:]:
+        fetch.wait()
 
     node = (me * chunk) // boards
     block = lax.rem(me, boards // chunk)
@@ -214,9 +241,10 @@
 
         @pl.when(t != me)
         def _():
-            gap_copy(t, me).start()
             sum_copy(t, me).start()
 
+    for step in range(1, depths):
+        gap_copy(lax.rem(me + step, depths), me).start()
     gap_recv[me] = gap_send[me]
     sum_recv[me] = sum_send[me]
 
@@ -290,9 +318,21 @@
     sizes = (depths, groups, boards, nodes, hands, width, chunk)
     cards, left, right = pair_tables(hands, width)
     vmem = pl.BlockSpec(memory_space=pltpu.VMEM)
-    smem = pl.BlockSpec(memory_space=pltpu.SMEM)
+    hbm = pl.BlockSpec(memory_space=pltpu.HBM)
     f32 = jnp.float32
     dma = pltpu.SemaphoreType.DMA
+    operands = (
+        root,
+        frontier,
+        regret_stop[0],
+        regret_go[0],
+        live,
+        board_cards.reshape(boards // chunk, chunk, -1),
+        rank.reshape(boards // chunk, chunk, hands),
+        cards,
+        left,
+        right,
+    )
     outs = pl.pallas_call(
         functools.partial(kernel, sizes),
         out_shape=(
@@ -300,9 +340,20 @@
             jax.ShapeDtypeStruct((boards, nodes, hands), f32),
             jax.ShapeDtypeStruct((2, nodes, hands), f32),
         ),
-        in_specs=[vmem] * 4 + [smem] + [vmem] * 5,
+        in_specs=[hbm] * 10,
         out_specs=(vmem, vmem, vmem),
         scratch_shapes=[
+            pltpu.VMEM((2, nodes, hands), f32),
+            pltpu.VMEM((2, nodes, hands), f32),
+            pltpu.VMEM((boards, nodes, hands), f32),
+            pltpu.VMEM((boards, nodes, hands), f32),
+            pltpu.SMEM((boards,), jnp.int32),
+            pltpu.VMEM((boards // chunk, chunk, board_cards.shape[1]), jnp.int32),
+            pltpu.VMEM((boards // chunk, chunk, hands), jnp.int32),
+            pltpu.VMEM(cards.shape, cards.dtype),
+            pltpu.VMEM(left.shape, left.dtype),
+            pltpu.VMEM(right.shape, right.dtype),
+            dma((10,)),
             pltpu.VMEM((depths, chunk, width), f32),
             pltpu.VMEM((depths, chunk, width), f32),
             pltpu.VMEM((depths, chunk, width), f32),
@@ -326,20 +377,9 @@
             dma((groups,)),
         ],
         compiler_params=pltpu.CompilerParams(
-            collective_id=0, has_side_effects=True, vmem_limit_bytes=56 * 1024 * 1024
+            collective_id=0, has_side_effects=True, vmem_limit_bytes=36 * 1024 * 1024
         ),
-    )(
-        root,
-        frontier,
-        regret_stop[0],
-        regret_go[0],
-        live,
-        board_cards.reshape(boards // chunk, chunk, -1),
-        rank.reshape(boards // chunk, chunk, hands),
-        cards,
-        left,
-        right,
-    )
+    )(*(pltpu.with_memory_space_constraint(operand, pltpu.HBM) for operand in operands))
     return tuple(out[None] for out in outs)
 
 

time: 33.1 us -> 27.4 us (0.83)
  Pallas kernels: 29 us -> 24.6 us
  local copies, waits for them, and re-layouts: 3.22 us -> 1.98 us
    pallas_call x1, Pallas kernels: 29 us -> 24.6 us  [local(): pl.pallas_call(functools.partial(kernel, sizes), out_shape=(jax.ShapeDtyp...]
    unnamed x7 -> x3, local copies, waits for them, and re-layouts: 3.22 us -> 1.98 us
where the time goes in v2:
time: 27.4 us; the launch traced here: 27.2 us
  Pallas kernels  24.6 us (90%)
  local copies, waits for them, and re-layouts  1.98 us (7%)
  between operations  0.64 us (2%)
    pallas_call x1, Pallas kernels, local(): pl.pallas_call(functools.partial(kernel, sizes), out_shape=(jax.ShapeDtyp...  24.6 us
    unnamed x3, local copies, waits for them, and re-layouts  1.98 us

profile of v2, /device:TPU:0, one launch (start us, length us, event | category | flops | bytes accessed | tf_op | source)
XLA Modules:
  0.0 27.2 jit_solution(7953014828470747534)
XLA Ops:
  0.6 24.6 %shard_map.121 = (f32[4,8,1326]{2,1,0:T(8,128)S(1)}, f32[4,8,1326]{2,1,0:T(8,128)S(1)}, f32[2,8,1326]{2,1,0:T(8,128)S(1)}) custom-call(f32[2,8,1326]{2,1,0:T(8,128)} %root_hbm.1, f32[2,8,1326]{2,1,0:T(8,128)} %frontier_hbm.1, f32[4,8,1326]{2,1,0:T(8,128)} %bitcast.10, f32[4,8,1326]{2,1,0:T(8,128)} %bitcast.11, s32[4]{0:T(128)} %live_hbm.1, ...), custom_call_target="tpu_custom_call" | custom-call | tf_op jit(solution)/shard_map/pallas_call | solution.py:336
  25.2 0.7 %copy.16 = f32[1,4,8,1326]{3,2,1,0:T(8,128)} copy(f32[1,4,8,1326]{3,2,1,0:T(8,128)S(1)} %bitcast.8) | data formatting | bytes 339456
  25.9 0.7 %copy.17 = f32[1,4,8,1326]{3,2,1,0:T(8,128)} copy(f32[1,4,8,1326]{3,2,1,0:T(8,128)S(1)} %bitcast.7) | data formatting | bytes 339456
  26.6 0.6 %copy.18 = f32[1,2,8,1326]{3,2,1,0:T(8,128)} copy(f32[1,2,8,1326]{3,2,1,0:T(8,128)S(1)} %bitcast.9) | data formatting | bytes 169728

commit v3 on v2

--- a/solution.py
+++ b/solution.py
@@ -30,6 +30,10 @@
         jnp.asarray(left, jnp.bfloat16),
         jnp.asarray(right, jnp.bfloat16),
     )
+
+
+def near_first(count):
+    return sorted(range(1, count), key=lambda step: (min(step, count - step), step))
 
 
 def kernel(
@@ -64,8 +68,6 @@
     gap_recv,
     sum_send,
     sum_recv,
-    part_send,
-    part_recv,
     free_pairs,
     payoff,
     reach_rows,
@@ -136,7 +138,7 @@
             device_id_type=MESH,
         )
 
-    for step in range(1, depths):
+    for step in reversed(near_first(depths)):
         go_copy(lax.rem(me + step, depths)).start()
     go_recv[me] = go_send[me]
 
@@ -151,14 +153,18 @@
     )
     rank = jnp.concatenate([rank, jnp.zeros((8 - chunk, width), jnp.float32)], axis=0)
     rank_col = jnp.transpose(rank)
-    free_pairs[...] = jnp.maximum(
+    pairs = jnp.maximum(
         jnp.dot(left_ref[...], right_ref[...], preferred_element_type=jnp.float32), 0.0
     ).astype(jnp.bfloat16)
+    free_pairs[0] = pairs
+    free_pairs[1] = -pairs
     for i in range(chunk):
         for top in range(0, width, LANES):
             diff = rank[i : i + 1, :] - rank_col[top : top + LANES, i : i + 1]
-            sign = jnp.clip(diff, -1.0, 1.0).astype(jnp.bfloat16)
-            payoff[i, top : top + LANES, :] = sign * free_pairs[top : top + LANES, :]
+            bounded = jnp.maximum(diff.astype(jnp.bfloat16), free_pairs[1, top : top + LANES, :])
+            payoff[i, top : top + LANES, :] = jnp.minimum(
+                bounded, free_pairs[0, top : top + LANES, :]
+            )
 
     lane = lax.broadcasted_iota(jnp.int32, (chunk, width), 1)
     mask = lane < hands
@@ -208,7 +214,7 @@
     def sum_copy(target, source):
         return pltpu.make_async_remote_copy(
             src_ref=sum_send.at[target],
-            dst_ref=sum_recv.at[source],
+            dst_ref=sum_recv.at[group, source],
             send_sem=send3.at[target],
             recv_sem=recv3.at[source],
             device_id={"section": target},
@@ -219,6 +225,10 @@
     alive = [
         jnp.where(live_ref[block * chunk + i] > 0, 1.0, 0.0) for i in range(chunk)
     ]
+    live_here = alive[0]
+    for i in range(1, chunk):
+        live_here = live_here + alive[i]
+    row_lane = lax.broadcasted_iota(jnp.int32, (1, width), 1)
     for t in reversed(range(depths)):
         q = t % 2
         go_t = go_recv[t]
@@ -237,44 +247,33 @@
             total = alive[0] * value[p][0:1]
             for i in range(1, chunk):
                 total = total + alive[i] * value[p][i : i + 1]
-            sum_send[t, p : p + 1, :] = total
+            sum_send[t, p : p + 1, :] = jnp.where(row_lane < hands, total, live_here)
 
         @pl.when(t != me)
         def _():
             sum_copy(t, me).start()
 
-    for step in range(1, depths):
+    for step in reversed(near_first(depths)):
         gap_copy(lax.rem(me + step, depths), me).start()
+    sum_recv[group, me] = sum_send[me]
     gap_recv[me] = gap_send[me]
-    sum_recv[me] = sum_send[me]
-
-    for step in range(1, depths):
-        sum_copy(0, lax.rem(me + depths - step, depths)).wait_recv()
-    per_node = boards // chunk
-    for n in range(nodes):
-        for p in range(2):
-            total = sum_recv[n * per_node, p : p + 1, :]
-            for extra in range(1, per_node):
-                total = total + sum_recv[n * per_node + extra, p : p + 1, :]
-            part_send[p, n : n + 1, :] = total
-    live_count = jnp.where(live_ref[0] > 0, 1.0, 0.0)
-    for j in range(1, boards):
-        live_count = live_count + jnp.where(live_ref[j] > 0, 1.0, 0.0)
-    part_send[:, :, hands:] = jnp.full((2, nodes, width - hands), 1.0, jnp.float32) * live_count
-
-    def part_copy(target, source):
+
+    def part_copy(target, at, source, node_source):
         return pltpu.make_async_remote_copy(
-            src_ref=part_send,
-            dst_ref=part_recv.at[source],
-            send_sem=send4.at[target],
-            recv_sem=recv4.at[source],
+            src_ref=sum_recv.at[source, node_source],
+            dst_ref=sum_recv.at[source, node_source],
+            send_sem=send4.at[target, node_source],
+            recv_sem=recv4.at[at, node_source],
             device_id={"board": target},
             device_id_type=MESH,
         )
 
-    for step in range(1, groups):
-        part_copy(lax.rem(group + step, groups), group).start()
-    part_recv[group] = part_send[...]
+    for step in [0] + near_first(depths):
+        source = lax.rem(me + step, depths)
+        if step:
+            sum_copy(0, source).wait_recv()
+        for hop in range(1, groups):
+            part_copy(lax.rem(group + hop, groups), group, group, source).start()
 
     for step in range(1, depths):
         gap_copy(0, lax.rem(me + depths - step, depths)).wait_recv()
@@ -295,12 +294,18 @@
         new_go_ref[j] = jnp.where(keep, new_go, go_now)
 
     for step in range(1, groups):
-        part_copy(0, lax.rem(group + groups - step, groups)).wait_recv()
-    for p in range(2):
-        total = part_recv[0, p]
-        for b in range(1, groups):
-            total = total + part_recv[b, p]
-        value_ref[p] = total[:, :hands] / total[:, hands : hands + 1]
+        source = lax.rem(group + step, groups)
+        for k in range(depths):
+            part_copy(source, source, source, k).wait_recv()
+    per_node = boards // chunk
+    for n in range(nodes):
+        total = jnp.zeros((2, width), jnp.float32)
+        for b in range(groups):
+            for k in range(n * per_node, (n + 1) * per_node):
+                total = total + sum_recv[b, k]
+        result = total[:, :hands] / total[:, hands : hands + 1]
+        for p in range(2):
+            value_ref[p, n : n + 1, :] = result[p : p + 1]
 
     for step in range(1, depths):
         peer = lax.rem(me + step, depths)
@@ -308,7 +313,21 @@
         gap_copy(peer, me).wait_send()
         sum_copy(peer, me).wait_send()
     for step in range(1, groups):
-        part_copy(lax.rem(group + step, groups), group).wait_send()
+        target = lax.rem(group + step, groups)
+        for k in range(depths):
+            part_copy(target, group, group, k).wait_send()
+
+
+def write_out(*refs):
+    sources, places, sem = refs[:3], refs[3:6], refs[6]
+    copies = [
+        pltpu.make_async_copy(source, place, sem.at[at])
+        for at, (source, place) in enumerate(zip(sources, places))
+    ]
+    for copy in copies:
+        copy.start()
+    for copy in copies:
+        copy.wait()
 
 
 def local(depths, groups, root, frontier, regret_stop, regret_go, live, board_cards, rank):
@@ -359,10 +378,8 @@
             pltpu.VMEM((depths, chunk, width), f32),
             pltpu.VMEM((depths, chunk, width), f32),
             pltpu.VMEM((depths, 2, width), f32),
-            pltpu.VMEM((depths, 2, width), f32),
-            pltpu.VMEM((2, nodes, width), f32),
-            pltpu.VMEM((groups, 2, nodes, width), f32),
-            pltpu.VMEM((width, width), jnp.bfloat16),
+            pltpu.VMEM((groups, depths, 2, width), f32),
+            pltpu.VMEM((2, width, width), jnp.bfloat16),
             pltpu.VMEM((chunk, width, width), jnp.bfloat16),
             pltpu.VMEM((chunk, 2 * depths, width), f32),
             pltpu.VMEM((chunk, 2 * depths, width), f32),
@@ -373,14 +390,22 @@
             dma((depths,)),
             dma((depths,)),
             dma((depths,)),
-            dma((groups,)),
-            dma((groups,)),
+            dma((groups, depths)),
+            dma((groups, depths)),
         ],
         compiler_params=pltpu.CompilerParams(
-            collective_id=0, has_side_effects=True, vmem_limit_bytes=36 * 1024 * 1024
+            collective_id=0, has_side_effects=True, vmem_limit_bytes=42 * 1024 * 1024
         ),
     )(*(pltpu.with_memory_space_constraint(operand, pltpu.HBM) for operand in operands))
-    return tuple(out[None] for out in outs)
+    whole = [out[None] for out in outs]
+    return pl.pallas_call(
+        write_out,
+        out_shape=tuple(jax.ShapeDtypeStruct(out.shape, f32) for out in whole),
+        in_specs=[pl.BlockSpec(memory_space=pl.ANY)] * 3,
+        out_specs=tuple(pl.BlockSpec(memory_space=pl.ANY) for _ in whole),
+        scratch_shapes=[dma((3,))],
+        compiler_params=pltpu.CompilerParams(vmem_limit_bytes=1024 * 1024),
+    )(*whole)
 
 
 def solution(mesh):

time: 27.4 us -> 25.9 us (0.945)
  local copies, waits for them, and re-layouts: 1.98 us -> 0 us
  Pallas kernels: 24.6 us -> 25.1 us
    unnamed x3 -> x0, local copies, waits for them, and re-layouts: 1.98 us -> none
    pallas_call x0 -> x1, Pallas kernels: none -> 0.79 us  [local(): pl.pallas_call(write_out, out_shape=tuple((jax.ShapeDtypeStruct(out.shape...]
    pallas_call x1, Pallas kernels: 24.6 us -> 24.3 us  [local(): pl.pallas_call(functools.partial(kernel, sizes), out_shape=(jax.ShapeDtyp...]
where the time goes in v3:
time: 25.9 us; the launch traced here: 25.7 us
  Pallas kernels  25.1 us (97%)
  between operations  0.64 us (2%)
    pallas_call x1, Pallas kernels, local(): pl.pallas_call(functools.partial(kernel, sizes), out_shape=(jax.ShapeDtyp...  24.3 us
    pallas_call x1, Pallas kernels, local(): pl.pallas_call(write_out, out_shape=tuple((jax.ShapeDtypeStruct(out.shape...  0.79 us

profile of v3, /device:TPU:0, one launch (start us, length us, event | category | flops | bytes accessed | tf_op | source)
XLA Modules:
  0.0 25.7 jit_solution(1953275909111038016)
XLA Ops:
  0.6 24.3 %shard_map.121 = (f32[4,8,1326]{2,1,0:T(8,128)S(1)}, f32[4,8,1326]{2,1,0:T(8,128)S(1)}, f32[2,8,1326]{2,1,0:T(8,128)S(1)}) custom-call(f32[2,8,1326]{2,1,0:T(8,128)} %root_hbm.1, f32[2,8,1326]{2,1,0:T(8,128)} %frontier_hbm.1, f32[4,8,1326]{2,1,0:T(8,128)} %bitcast.10, f32[4,8,1326]{2,1,0:T(8,128)} %bitcast.11, s32[4]{0:T(128)} %live_hbm.1, ...), custom_call_target="tpu_custom_call" | custom-call | tf_op jit(solution)/shard_map/pallas_call | solution.py:355
  24.9 0.8 %shard_map.122 = (f32[1,4,8,1326]{3,2,1,0:T(8,128)}, f32[1,4,8,1326]{3,2,1,0:T(8,128)}, f32[1,2,8,1326]{3,2,1,0:T(8,128)}) custom-call(f32[1,4,8,1326]{3,2,1,0:T(8,128)S(1)} %bitcast.7, f32[1,4,8,1326]{3,2,1,0:T(8,128)S(1)} %bitcast.8, f32[1,2,8,1326]{3,2,1,0:T(8,128)S(1)} %bitcast.9), custom_call_target="tpu_custom_call" | custom-call | tf_op jit(solution)/shard_map/pallas_call | solution.py:401

commit v4 on v3

--- a/solution.py
+++ b/solution.py
@@ -73,6 +73,7 @@
     reach_rows,
     leaf_rows,
     gap_home,
+    prob_home,
     send1,
     recv1,
     send2,
@@ -112,6 +113,7 @@
         stop_now = stop_ref[j]
         go_now = go_ref[j]
         go_prob = go_now / (stop_now + go_now)
+        prob_home[j] = go_prob
         for n in range(nodes):
             unit = n * boards + j
             go_send[unit // chunk, unit % chunk : unit % chunk + 1, :hands] = go_prob[n : n + 1]
@@ -181,11 +183,13 @@
 
     reach = [node_row(root_ref, p) for p in range(2)]
 
-    for step in range(1, depths):
-        go_arrival(lax.rem(me + depths - step, depths)).wait_recv()
-
     for t in range(depths):
         q = t % 2
+
+        @pl.when(t != me)
+        def _():
+            go_arrival(t).wait_recv()
+
         go_t = go_recv[t]
         weighted = [reach[0], reach[1]]
         weighted[q] = reach[q] * (1.0 - go_t)
@@ -253,8 +257,6 @@
         def _():
             sum_copy(t, me).start()
 
-    for step in reversed(near_first(depths)):
-        gap_copy(lax.rem(me + step, depths), me).start()
     sum_recv[group, me] = sum_send[me]
     gap_recv[me] = gap_send[me]
 
@@ -274,6 +276,9 @@
             sum_copy(0, source).wait_recv()
         for hop in range(1, groups):
             part_copy(lax.rem(group + hop, groups), group, group, source).start()
+
+    for step in reversed(near_first(depths)):
+        gap_copy(lax.rem(me + step, depths), me).start()
 
     for step in range(1, depths):
         gap_copy(0, lax.rem(me + depths - step, depths)).wait_recv()
@@ -285,11 +290,11 @@
     for j in range(boards):
         stop_now = stop_ref[j]
         go_now = go_ref[j]
-        total = stop_now + go_now
+        go_prob = prob_home[j]
         keep = live_ref[j] > 0
         gap = gap_home[j][:, :hands]
-        new_stop = jnp.maximum(stop_now + (go_now / total) * gap, 0.0)
-        new_go = jnp.maximum(go_now - (stop_now / total) * gap, 0.0)
+        new_stop = jnp.maximum(stop_now + go_prob * gap, 0.0)
+        new_go = jnp.maximum(go_now - (1.0 - go_prob) * gap, 0.0)
         new_stop_ref[j] = jnp.where(keep, new_stop, stop_now)
         new_go_ref[j] = jnp.where(keep, new_go, go_now)
 
@@ -384,6 +389,7 @@
             pltpu.VMEM((chunk, 2 * depths, width), f32),
             pltpu.VMEM((chunk, 2 * depths, width), f32),
             pltpu.VMEM((boards, nodes, width), f32),
+            pltpu.VMEM((boards, nodes, hands), f32),
             dma((depths,)),
             dma((depths,)),
             dma((depths,)),

time: 25.9 us -> 25.3 us (0.977)
  Pallas kernels: 25.1 us -> 24.5 us
    pallas_call x1, Pallas kernels: 24.3 us -> 23.7 us  [local(): pl.pallas_call(functools.partial(kernel, sizes), out_shape=(jax.ShapeDtyp...]
where the time goes in v4:
time: 25.3 us; the launch traced here: 25.2 us
  Pallas kernels  24.5 us (97%)
  between operations  0.64 us (3%)
    pallas_call x1, Pallas kernels, local(): pl.pallas_call(functools.partial(kernel, sizes), out_shape=(jax.ShapeDtyp...  23.7 us
    pallas_call x1, Pallas kernels, local(): pl.pallas_call(write_out, out_shape=tuple((jax.ShapeDtypeStruct(out.shape...  0.79 us

profile of v4, /device:TPU:0, one launch (start us, length us, event | category | flops | bytes accessed | tf_op | source)
XLA Modules:
  0.0 25.2 jit_solution(10607643888695172558)
XLA Ops:
  0.6 23.7 %shard_map.121 = (f32[4,8,1326]{2,1,0:T(8,128)S(1)}, f32[4,8,1326]{2,1,0:T(8,128)S(1)}, f32[2,8,1326]{2,1,0:T(8,128)S(1)}) custom-call(f32[2,8,1326]{2,1,0:T(8,128)} %root_hbm.1, f32[2,8,1326]{2,1,0:T(8,128)} %frontier_hbm.1, f32[4,8,1326]{2,1,0:T(8,128)} %bitcast.10, f32[4,8,1326]{2,1,0:T(8,128)} %bitcast.11, s32[4]{0:T(128)} %live_hbm.1, ...), custom_call_target="tpu_custom_call" | custom-call | tf_op jit(solution)/shard_map/pallas_call | solution.py:360
  24.4 0.8 %shard_map.122 = (f32[1,4,8,1326]{3,2,1,0:T(8,128)}, f32[1,4,8,1326]{3,2,1,0:T(8,128)}, f32[1,2,8,1326]{3,2,1,0:T(8,128)}) custom-call(f32[1,4,8,1326]{3,2,1,0:T(8,128)S(1)} %bitcast.7, f32[1,4,8,1326]{3,2,1,0:T(8,128)S(1)} %bitcast.8, f32[1,2,8,1326]{3,2,1,0:T(8,128)S(1)} %bitcast.9), custom_call_target="tpu_custom_call" | custom-call | tf_op jit(solution)/shard_map/pallas_call | solution.py:407
